TPU v7x, 32 devices: a 4x2x2 block of a 4x4x8 slice. The times are simulated.
32 devices in a mesh: dp: 4 (over y, z), tp: 8 (over x, core).
Axes of the slice: x: 4, y: 2, z: 2, core: 2. Of those that a mesh axis runs over, the one named last changes fastest.
The devices are a block of a 4x4x8 slice.
Arguments:
- hidden: bfloat16 [24, 8, 4096], P('dp'), parts along dimension 0
- draft_ids: int32 [24, 7], P('dp'), parts along dimension 0
- temperature: float32 [24], P('dp'), parts along dimension 0
- norm_gain: bfloat16 [4096], replicated
- head_weight: bfloat16 [128256, 4096], P('tp')
Outputs:
- output 1: float32 [24, 7], P('dp'), parts along dimension 0
- output 2: float32 [24, 8], P('dp'), parts along dimension 0
- output 3: float32 [24, 8], P('dp'), parts along dimension 0
There are 4 independent parts. A program takes and returns all parts, laid end to end along the dimension named above; an argument that names none is the same for every part.
All inputs are finite; a program needn't handle non-finite values.
Results may differ from a plain program's by a relative error of at most 0.001.
Values sent between devices are 32-bit elements.
A program may use at most 768 MiB of HBM per device.

v0:
```python
import jax
import jax.numpy as jnp
from jax import lax
from jax.sharding import PartitionSpec as P, NamedSharding

NORM_EPS = 1e-5


def solution(mesh):
    def local_step(hidden, draft_ids, value_a11, norm_gain, head_shard):
        draft_len = draft_ids.shape[1]
        hidden_f32 = hidden.astype(jnp.float32)
        mean_sq = jnp.mean(hidden_f32 * hidden_f32, axis=-1, keepdims=True)
        normed = (hidden_f32 * lax.rsqrt(mean_sq + NORM_EPS) * norm_gain.astype(jnp.float32)).astype(jnp.bfloat16)
        shard_logits = jnp.einsum("bpd,vd->bpv", normed, head_shard, preferred_element_type=jnp.float32)
        shard_logits = shard_logits / value_a11[:, None, None]
        logits = lax.all_gather(shard_logits, "tp", axis=2, tiled=True)
        row_max = jnp.max(logits, axis=-1, keepdims=True)
        shifted = jnp.exp(logits - row_max)
        total = jnp.sum(shifted, axis=-1)
        weighted = jnp.sum(shifted * logits, axis=-1)
        log_norm = row_max[..., 0] + jnp.log(total)
        entropy = log_norm - weighted / total
        picked = jnp.take_along_axis(logits[:, :draft_len], draft_ids[:, :, None], axis=2)[..., 0]
        return picked - log_norm[:, :draft_len], log_norm, entropy

    return jax.shard_map(
        local_step,
        mesh=mesh,
        in_specs=(P("dp", None, None), P("dp", None), P("dp"), P(None), P("tp", None)),
        out_specs=(P("dp", None), P("dp", None), P("dp", None)),
        check_vma=False,
    )
```

profile of v0, /device:TPU:81, one launch (start us, length us, event | category | flops | bytes accessed | tf_op | source)
XLA Modules:
  0.0 2911.7 jit_solution(11473236376937401341)
XLA Ops:
  7.2 0.1 all-gather.2.cloned.1.call-start
  7.2 0.7 convert_element_type.10
  7.9 1.2 fusion.6
  9.1 0.0 copy-start.2
  9.1 48.6 %fusion.3 = f32[6,8,16032]{2,1,0:T(8,128)S(1)} fusion(bf16[16032,4096]{1,0:T(8,128)(2,1)} %param.9, f32[6]{0:T(128)} %param.7, bf16[6,8,4096]{2,1,0:T(8,128)(2,1)} %param.5, f32[4096]{0:T(1024)S(1)} %convert_element_type.10, f32[6,8]{1,0:T(8,128)S(1)} %add_rsqrt_fusion), kind=kOutput, calls=%fused_computation.6 | convolution fusion | flops 6305594880 | bytes 134822112 | tf_op jit(solution)/shard_map/bpd,vd->bpv/dot_general | solution.py:15
  57.7 29.7 %copy.8 = f32[6,8,16032]{1,0,2:T(8,128)} copy(f32[6,8,16032]{2,1,0:T(8,128)S(1)} %fusion.3) | data formatting | bytes 6156288 | tf_op jit(solution)/shard_map/div | solution.py:16
  87.5 0.1 all-gather.2.cloned.1.call-update
  87.5 0.0 copy-done.2
  87.6 0.6 reshape.42
  88.2 2222.5 %all-gather.2.cloned.1.call-done = f32[6,8,128256]{1,0,2:T(8,128)} async-done(((f32[6,8,16032]{1,0,2:T(8,128)}), f32[6,8,128256]{1,0,2:T(8,128)}) %all-gather.2.cloned.1.call-update) | async-done | bytes 24625168 | tf_op jit(solution)/shard_map/all_gather | solution.py:17
  2310.7 0.0 copy-start
  2310.7 257.8 %copy.10 = f32[6,7,128256]{2,1,0:T(8,128)} copy(f32[6,7,128256]{1,0,2:T(8,128)} %bitcast.12) | data formatting | bytes 43094016
  2568.5 0.0 copy-done
  2568.5 2.1 gather_fusion
  2570.6 0.7 gather.7
  2571.3 156.8 %reduce_max.9 = f32[6,8]{1,0:T(8,128)S(1)} reduce(f32[6,8,128256]{1,0,2:T(8,128)} %all-gather.2.cloned.1.call-done, f32[]{:T(128)} %constant.24.clone.1), dimensions={2}, to_apply=%region_1.0 | reduce | flops 6156240 | bytes 24625348 | tf_op jit(solution)/shard_map/reduce_max | solution.py:18
  2728.1 0.0 copy-start.3
  2728.1 0.0 copy-start.4
  2728.1 175.5 %multiply_reduce_fusion = (f32[6,8]{1,0:T(8,128)S(1)}, f32[6,8]{1,0:T(8,128)S(1)}) fusion(f32[6,8,128256]{1,0,2:T(8,128)} %all-gather.2.cloned.1.call-done, f32[6,8]{1,0:T(8,128)S(1)} %reduce_max.9), kind=kLoop, calls=%fused_computation.1 | loop fusion | flops 24625056 | bytes 24625728 | tf_op jit(solution)/shard_map/reduce_sum | solution.py:21
  2903.6 0.6 divide_subtract_fusion
  2904.2 0.0 copy-start.1
  2904.2 0.0 copy-done.3
  2904.2 0.0 copy-done.4
  2904.2 0.6 slice_subtract_fusion
  2904.8 0.0 copy-done.1
  (6 shorter events, 0.0 us)
Async XLA Ops:
  7.2 2303.5 %all-gather.2.cloned.1.call-start = ((), (), s32[]{:S(2)}) async-start(), calls=%async_computation | async-start | bytes 591003648 | tf_op jit(solution)/shard_map/all_gather | solution.py:17
  9.1 78.4 %copy-start.2 = (s32[6,7]{1,0:T(8,128)S(1)}, s32[6,7]{1,0:T(8,128)}, u32[]{:S(2)}) copy-start(s32[6,7]{1,0:T(8,128)} %param.6) | copy-start | bytes 508
  2310.7 257.9 %copy-start = (s32[42]{0:T(128)S(1)}, s32[42]{0:T(128)}, u32[]{:S(2)}) copy-start(s32[42]{0:T(128)} %reshape.42) | copy-start | bytes 508
  2728.1 176.1 %copy-start.3 = (s32[6,7]{1,0:T(8,128)S(1)}, s32[6,7]{1,0:T(8,128)}, u32[]{:S(2)}) copy-start(s32[6,7]{1,0:T(8,128)} %param.6) | copy-start | bytes 508
  2728.1 176.1 %copy-start.4 = (f32[6,7]{1,0:T(8,128)S(1)}, f32[6,7]{1,0:T(8,128)}, u32[]{:S(2)}) copy-start(f32[6,7]{1,0:T(8,128)} %gather.7) | copy-start | bytes 508
  2904.2 0.6 copy-start.1
Sparse Core Ops, SparseCore 0:
  87.7 2222.9 all-gather.1
where the time goes:
time: 2920 us; the launch traced here: 2910 us
  waiting for transfers between devices  2220 us (76%)
  other arithmetic  335 us (11%)
  local copies, waits for them, and re-layouts  291 us (10%)
  matrix products  48.6 us (2%)
    all_gather x1, waiting for transfers between devices, local_step(): logits = lax.all_gather(shard_logits, 'tp', axis=2, tiled=True)  2220 us
    unnamed x13, local copies, waits for them, and re-layouts  258 us
    reduce_sum x1, other arithmetic, local_step(): weighted = jnp.sum(shifted * logits, axis=-1)  175 us
    reduce_max x1, other arithmetic, local_step(): row_max = jnp.max(logits, axis=-1, keepdims=True)  157 us
  transfers between devices with their start and end apart: 1, of which 1 were waited for; matrix products, arithmetic and copies ran while one was open for 0% of the time, Pallas kernels for 0%

commit v1 on v0

v1 whole, which is shorter than its diff:
```python
import functools

import jax
import jax.numpy as jnp
from jax import lax
from jax.experimental import pallas as pl
from jax.experimental.pallas import tpu as pltpu
from jax.sharding import PartitionSpec as P

NORM_EPS = 1e-5
TILE = 1024
SLOTS = 5
LANES = 128
LOW = -1e30


def norm_rows(h_ref, gain_ref, g_ref):
    x = h_ref[...].astype(jnp.float32)
    inv = lax.rsqrt(jnp.mean(x * x, axis=-1, keepdims=True) + NORM_EPS)
    gain = gain_ref[...].astype(jnp.float32)
    for k in range(gain.shape[0]):
        cols = slice(k * LANES, (k + 1) * LANES)
        g_ref[:, cols] = (x[:, cols] * inv * gain[k:k + 1, :]).astype(jnp.bfloat16)


def row_tables(draft_ref, temp_ref, dl_ref, it_ref, first, rows, pos):
    batch, drafts = draft_ref.shape
    sub = lax.broadcasted_iota(jnp.int32, (pos, LANES), 0)
    lane = lax.broadcasted_iota(jnp.int32, (pos, LANES), 1)
    none = -(1 << 24)
    for b in range(batch):
        ids = jnp.broadcast_to(draft_ref[b:b + 1, :].astype(jnp.float32), (pos, drafts))
        own = jnp.where(sub[:, :drafts] == lane[:, :drafts], ids, 0.0)
        col = jnp.sum(own, axis=1, keepdims=True).astype(jnp.int32) - first
        col = jnp.broadcast_to(col, (pos, LANES))
        ok = (col >= 0) & (col < rows) & (sub < drafts)
        dl_ref[b * pos:(b + 1) * pos, :] = jnp.where(ok, col, none)
        temps = jnp.broadcast_to(temp_ref[...], (pos, batch))
        temps = jnp.sum(jnp.where(lane[:, :batch] == b, temps, 0.0), axis=1, keepdims=True)
        it_ref[b * pos:(b + 1) * pos, :] = jnp.broadcast_to(1.0 / temps, (pos, LANES))


def fold_tile(z_ref, width, first, valid, it_ref, dl_ref, m_ref, s_ref, t_ref, p_ref):
    lane = lax.broadcasted_iota(jnp.int32, m_ref.shape, 1)
    scale = it_ref[...]
    wanted = dl_ref[...] - first - lane
    cols = []
    for j in range(width // LANES):
        z = z_ref[:, j * LANES:(j + 1) * LANES] * scale
        if (j + 1) * LANES > valid:
            z = jnp.where(lane < valid - j * LANES, z, 2 * LOW)
        cols.append(z)
    m_old = m_ref[...]
    m_new = m_old
    for z in cols:
        m_new = jnp.maximum(m_new, z)
    alpha = jnp.exp(m_old - m_new)
    s = s_ref[...] * alpha
    t = t_ref[...] * alpha
    p = p_ref[...]
    for j, z in enumerate(cols):
        e = jnp.exp(z - m_new)
        s = s + e
        t = t + e * z
        p = p + jnp.where(wanted == j * LANES, z, 0.0)
    m_ref[...] = m_new
    s_ref[...] = s
    t_ref[...] = t
    p_ref[...] = p


def pack(m_ref, s_ref, t_ref, p_ref, batch, pos):
    sub = lax.broadcasted_iota(jnp.int32, (pos, LANES), 0)
    lane = lax.broadcasted_iota(jnp.int32, (pos, LANES), 1)
    diff = lane - sub
    out_row = lax.broadcasted_iota(jnp.int32, (8, LANES), 0)
    packed = jnp.zeros((8, LANES), jnp.float32)
    for b in range(batch):
        rows = pl.ds(b * pos, pos)
        m = m_ref[rows, :]
        top = jnp.max(m, axis=1, keepdims=True)
        w = jnp.exp(m - top)
        s = jnp.sum(s_ref[rows, :] * w, axis=1, keepdims=True)
        t = jnp.sum(t_ref[rows, :] * w, axis=1, keepdims=True)
        p = jnp.sum(p_ref[rows, :], axis=1, keepdims=True)
        v = jnp.where(diff == 0, s, 0.0)
        v = v + jnp.where(diff == 8, t, 0.0)
        v = v + jnp.where(diff == 16, p, 0.0)
        v = v + jnp.where((diff == 64) | (diff == 72), top, 0.0)
        v = jnp.sum(v, axis=0, keepdims=True)
        packed = jnp.where(out_row == b, v, packed)
    return packed


def kernel(tp, batch, pos, h_hbm, draft_hbm, temp_hbm, gain_hbm, w_ref, out_ref,
           h_ref, draft_ref, temp_ref, gain_ref, dl_ref, it_ref, g_ref, w_buf, w_tail, z_ref, m_ref, s_ref, t_ref, p_ref, send_buf, recv_buf,
           in_sem, w_sem, tail_sem, send_sem, recv_sem):
    rows = w_ref.shape[0]
    n_full = rows // TILE
    tail = rows - n_full * TILE
    me = lax.axis_index("tp")

    def fetch(i, slot):
        return pltpu.make_async_copy(
            w_ref.at[pl.ds(pl.multiple_of(i * TILE, TILE), TILE), :], w_buf.at[slot], w_sem.at[slot])

    tail_copy = pltpu.make_async_copy(
        w_ref.at[pl.ds(n_full * TILE, tail), :], w_tail.at[pl.ds(0, tail), :], tail_sem)

    inputs = [pltpu.make_async_copy(src, dst, in_sem.at[i]) for i, (src, dst) in enumerate(
        ((h_hbm, h_ref), (draft_hbm, draft_ref), (temp_hbm, temp_ref), (gain_hbm, gain_ref)))]
    for copy in inputs:
        copy.start()
    for i in range(SLOTS):
        fetch(i, i).start()

    barrier = pltpu.get_barrier_semaphore()
    for k in range(1, tp):
        pl.semaphore_signal(barrier, inc=1, device_id={"tp": lax.rem(me + k, tp)},
                            device_id_type=pl.DeviceIdType.MESH)

    for copy in inputs:
        copy.wait()
    norm_rows(h_ref, gain_ref, g_ref)
    row_tables(draft_ref, temp_ref, dl_ref, it_ref, me * rows, rows, pos)
    m_ref[...] = jnp.full(m_ref.shape, LOW, jnp.float32)
    s_ref[...] = jnp.zeros(s_ref.shape, jnp.float32)
    t_ref[...] = jnp.zeros(t_ref.shape, jnp.float32)
    p_ref[...] = jnp.zeros(p_ref.shape, jnp.float32)
    z_ref[...] = jnp.full(z_ref.shape, 2 * LOW, jnp.float32)
    pad = w_tail.shape[0] - tail
    if pad:
        w_tail[pl.ds(tail, pad), :] = jnp.zeros((pad, w_tail.shape[1]), jnp.bfloat16)

    def dot(w):
        return lax.dot_general(g_ref[...], w, (((1,), (1,)), ((), ())), preferred_element_type=jnp.float32)

    stats = (it_ref, dl_ref, m_ref, s_ref, t_ref, p_ref)

    def step(i, _):
        slot = lax.rem(i, SLOTS)
        fetch(i, slot).wait()
        fold_tile(z_ref, TILE, (i - 1) * TILE, TILE, *stats)
        z_ref[...] = dot(w_buf[slot])

        @pl.when(i + SLOTS < n_full)
        def _():
            fetch(i + SLOTS, slot).start()

        @pl.when(i + SLOTS == n_full)
        def _():
            tail_copy.start()

        return 0

    lax.fori_loop(0, n_full, step, 0)
    fold_tile(z_ref, TILE, (n_full - 1) * TILE, TILE, *stats)
    tail_copy.wait()
    width = w_tail.shape[0]
    z_ref[:, pl.ds(0, width)] = dot(w_tail[...])
    fold_tile(z_ref, width, n_full * TILE, tail, *stats)

    packed = pack(m_ref, s_ref, t_ref, p_ref, batch, pos)
    send_buf[...] = packed
    recv_buf[me] = packed
    pl.semaphore_wait(barrier, tp - 1)
    copies = []
    for k in range(1, tp):
        copy = pltpu.make_async_remote_copy(
            src_ref=send_buf, dst_ref=recv_buf.at[me], send_sem=send_sem.at[k - 1],
            recv_sem=recv_sem.at[k - 1], device_id={"tp": lax.rem(me + k, tp)},
            device_id_type=pl.DeviceIdType.MESH)
        copy.start()
        copies.append(copy)
    for copy in copies:
        copy.wait()

    parts = [recv_buf[k] for k in range(tp)]
    tops = [pltpu.roll(v, 64, 1) for v in parts]
    top = functools.reduce(jnp.maximum, tops)
    acc = jnp.zeros_like(packed)
    for v, m in zip(parts, tops):
        acc = acc + v * jnp.exp(m - top)
    t_al = pltpu.roll(acc, LANES - 8, 1)
    p_al = pltpu.roll(acc, LANES - 16, 1)
    log_norm = top[:, :pos] + jnp.log(acc[:, :pos])
    out_ref[:, 0:pos] = log_norm
    out_ref[:, 8:8 + pos] = log_norm - t_al[:, :pos] / acc[:, :pos]
    out_ref[:, 16:16 + pos] = p_al[:, :pos] - log_norm


def solution(mesh):
    tp = mesh.shape["tp"]

    def local_step(hidden, draft_ids, temperature, norm_gain, head_shard):
        batch, pos, dim = hidden.shape
        rows = head_shard.shape[0]
        n_rows = batch * pos
        tail = rows % TILE
        tail_pad = -(-tail // 256) * 256
        vmem = pl.BlockSpec(memory_space=pltpu.VMEM)
        stat = pltpu.VMEM((n_rows, LANES), jnp.float32)
        out = pl.pallas_call(
            functools.partial(kernel, tp, batch, pos),
            out_shape=jax.ShapeDtypeStruct((8, LANES), jnp.float32),
            in_specs=[pl.BlockSpec(memory_space=pltpu.HBM)] * 5,
            out_specs=vmem,
            scratch_shapes=[
                pltpu.VMEM((n_rows, dim), jnp.bfloat16),
                pltpu.VMEM(draft_ids.shape, jnp.int32),
                pltpu.VMEM((1, batch), jnp.float32),
                pltpu.VMEM((dim // LANES, LANES), jnp.bfloat16),
                pltpu.VMEM((n_rows, LANES), jnp.int32),
                stat,
                pltpu.VMEM((n_rows, dim), jnp.bfloat16),
                pltpu.VMEM((SLOTS, TILE, dim), jnp.bfloat16),
                pltpu.VMEM((tail_pad, dim), jnp.bfloat16),
                pltpu.VMEM((n_rows, TILE), jnp.float32),
                stat, stat, stat, stat,
                pltpu.VMEM((8, LANES), jnp.float32),
                pltpu.VMEM((tp, 8, LANES), jnp.float32),
                pltpu.SemaphoreType.DMA((4,)),
                pltpu.SemaphoreType.DMA((SLOTS,)),
                pltpu.SemaphoreType.DMA,
                pltpu.SemaphoreType.DMA((tp - 1,)),
                pltpu.SemaphoreType.DMA((tp - 1,)),
            ],
            compiler_params=pltpu.CompilerParams(
                collective_id=0, has_side_effects=True, vmem_limit_bytes=60 * 1024 * 1024),
        )(hidden.reshape(n_rows, dim), draft_ids, temperature.reshape(1, batch),
          norm_gain.reshape(dim // LANES, LANES), head_shard)
        return out[:batch, 16:16 + pos - 1], out[:batch, :pos], out[:batch, 8:8 + pos]

    return jax.shard_map(
        local_step,
        mesh=mesh,
        in_specs=(P("dp", None, None), P("dp", None), P("dp"), P(None), P("tp", None)),
        out_specs=(P("dp", None), P("dp", None), P("dp", None)),
        check_vma=False,
    )
```

time: 2920 us -> 63 us (0.02)
  waiting for transfers between devices: 2220 us -> 0 us
  other arithmetic: 335 us -> 0 us
  local copies, waits for them, and re-layouts: 291 us -> 2.75 us
  Pallas kernels: 0 us -> 59.4 us
  matrix products: 48.6 us -> 0 us
    all_gather x1 -> x0, waiting for transfers between devices: 2220 us -> none  [local_step(): logits = lax.all_gather(shard_logits, 'tp', axis=2, tiled=True)]
    unnamed x13 -> x0, local copies, waits for them, and re-layouts: 258 us -> none
    reduce_sum x2 -> x0, other arithmetic: 177 us -> none  [the longest x1 175 us: local_step(): weighted = jnp.sum(shifted * logits, axis=-1)]
    reduce_max x1 -> x0, other arithmetic: 157 us -> none  [local_step(): row_max = jnp.max(logits, axis=-1, keepdims=True)]
    pallas_call x0 -> x1, Pallas kernels: none -> 59.4 us  [local_step(): pl.pallas_call(functools.partial(kernel, tp, batch, pos), out_shape=jax.S...]
    dot_general x1 -> x0, matrix products: 48.6 us -> none  [local_step(): jnp.einsum('bpd,vd->bpv', normed, head_shard, preferred_element_type=jnp....]
    div x1 -> x0, local copies, waits for them, and re-layouts: 29.7 us -> none  [local_step(): shard_logits = shard_logits / value_a11[:, None, None]]
  transfers between devices with their start and end apart: 1 -> 0, of which waited for: 1 -> 0; matrix products, arithmetic and copies ran while one was open for 0% -> 0% of each run, Pallas kernels for 0% -> 0%
where the time goes in v1:
time: 63 us; the launch traced here: 62.8 us
  Pallas kernels  59.4 us (94%)
  local copies, waits for them, and re-layouts  2.75 us (4%)
  between operations  0.64 us (1%)
    pallas_call x1, Pallas kernels, local_step(): pl.pallas_call(functools.partial(kernel, tp, batch, pos), out_shape=jax.S...  59.4 us
    slice x1, local copies, waits for them, and re-layouts, local_step(): out[:batch, 8:8 + pos]  1.41 us
    slice x1, local copies, waits for them, and re-layouts, local_step(): out[:batch, 16:16 + pos - 1]  1.33 us

profile of v1, /device:TPU:81, one launch (start us, length us, event | category | flops | bytes accessed | tf_op | source)
XLA Modules:
  0.0 62.8 jit_solution(14100048794123709747)
XLA Ops:
  0.6 59.4 %shard_map.76 = f32[8,128]{1,0:T(8,128)} custom-call(bf16[48,4096]{1,0:T(8,128)(2,1)} %bitcast.3, s32[6,7]{1,0:T(8,128)} %draft_hbm.1, f32[1,6]{1,0:T(1,128)} %bitcast.5, bf16[32,128]{1,0:T(8,128)(2,1)} %bitcast.4, bf16[16032,4096]{1,0:T(8,128)(2,1)} %w_ref.1), custom_call_target="tpu_custom_call" | custom-call | tf_op jit(solution)/shard_map/pallas_call | solution.py:203
  60.0 1.4 %fusion = (f32[6,8]{1,0:T(8,128)}, f32[6,8]{1,0:T(8,128)}) fusion(f32[8,128]{1,0:T(8,128)} %shard_map.76), kind=kLoop, calls=%fused_computation | loop fusion | bytes 768 | tf_op jit(solution)/shard_map/slice | solution.py:232
  61.4 1.3 %slice.9 = f32[6,7]{1,0:T(8,128)} slice(f32[8,128]{1,0:T(8,128)} %shard_map.76), slice={[0:6], [16:23]} | slice | bytes 336 | tf_op jit(solution)/shard_map/slice | solution.py:232

commit v2 on v0

v2 whole, which is shorter than its diff:
```python
import functools

import jax
import jax.numpy as jnp
from jax import lax
from jax.experimental import pallas as pl
from jax.experimental.pallas import tpu as pltpu
from jax.sharding import PartitionSpec as P

NORM_EPS = 1e-5
PAIR = True
TILE = 512
SLOTS = 10
OWN_TILES = 9
FORWARD_AT = (4, 6, 8)
LANES = 128
SUBS = 8
LOW = -1e30
MESH = pl.DeviceIdType.MESH


def norm_rows(h_ref, gain_ref, g_ref):
    x = h_ref[...].astype(jnp.float32)
    inv = lax.rsqrt(jnp.mean(x * x, axis=-1, keepdims=True) + NORM_EPS)
    gain = gain_ref[...].astype(jnp.float32)
    batch, pos, _ = g_ref.shape
    for k in range(gain.shape[0]):
        cols = slice(k * LANES, (k + 1) * LANES)
        g = (x[:, cols] * inv * gain[k:k + 1, :]).astype(jnp.bfloat16).astype(jnp.float32)
        for b in range(batch):
            g_ref[b, :, cols] = g[b * pos:(b + 1) * pos, :]


def transpose_rows(sources, gt_ref):
    batch, pos, dim = sources[0].shape
    used = len(sources) * batch * pos
    for k in range(dim // LANES):
        cols = slice(k * LANES, (k + 1) * LANES)
        rows = [src[b, :, cols] for src in sources for b in range(batch)]
        rows.append(jnp.zeros((LANES - used, LANES), jnp.float32))
        gt_ref[cols, :] = jnp.concatenate(rows, axis=0).T.astype(jnp.bfloat16)


def fold_tile(z_ref, width, first, scale, draft, m_ref, s_ref, t_ref, p_ref):
    wanted = draft - first - lax.broadcasted_iota(jnp.int32, (SUBS, LANES), 0)
    count = width // SUBS

    def chunk(r):
        return z_ref[r * SUBS:(r + 1) * SUBS, :] * scale

    ways = 4
    tops = [m_ref[...]] * ways
    m_old = tops[0]
    for r in range(count):
        tops[r % ways] = jnp.maximum(tops[r % ways], chunk(r))
    m_new = functools.reduce(jnp.maximum, tops)
    alpha = jnp.exp(m_old - m_new)
    zero = jnp.zeros_like(m_old)
    s = [s_ref[...] * alpha] + [zero] * (ways - 1)
    t = [t_ref[...] * alpha] + [zero] * (ways - 1)
    p = [p_ref[...]] + [zero] * (ways - 1)
    for r in range(count):
        z = chunk(r)
        e = jnp.exp(z - m_new)
        w = r % ways
        s[w] = s[w] + e
        t[w] = t[w] + e * z
        p[w] = p[w] + jnp.where(wanted == r * SUBS, z, 0.0)
    m_ref[...] = m_new
    s_ref[...] = sum(s[1:], s[0])
    t_ref[...] = sum(t[1:], t[0])
    p_ref[...] = sum(p[1:], p[0])


def kernel(tp, pair, batch, pos, own, half, h_hbm, draft_hbm, temp_hbm, gain_hbm, w_ref, out_ref,
           h_ref, draft_ref, temp_ref, gain_ref, table_ref, other_table_ref, g_ref, other_ref, gt_ref, w_buf, w_tail, z_ref,
           scale_ref, want_ref, m_ref, s_ref, t_ref, p_ref, msg_ref, inbox_ref,
           in_sem, w_sem, tail_sem, send_sem, recv_sem, pass_sem, got_sem, out_sem, msg_sem):
    rows = w_ref.shape[0]
    used = batch * pos
    me = lax.axis_index("tp")
    dp = lax.axis_index("dp")
    mate = dp + 1 - 2 * lax.rem(dp, 2)
    core = lax.rem(me, 2)
    twin = me + 1 - 2 * core
    n_full = own + half // TILE
    tail = half % TILE
    skip = lax.rem(dp, 2) * half if pair else 0

    def own_tile(i, slot):
        start = pl.multiple_of(i * TILE, TILE)
        return pltpu.make_async_copy(w_ref.at[pl.ds(start, TILE), :], w_buf.at[slot], w_sem.at[slot])

    def shared_tile(i, slot):
        start = pl.multiple_of(i * TILE + skip, 16)
        return pltpu.make_async_copy(w_ref.at[pl.ds(start, TILE), :], w_buf.at[slot], w_sem.at[slot])

    tail_start = pl.multiple_of(n_full * TILE + skip, 16)
    tail_copy = pltpu.make_async_copy(w_ref.at[pl.ds(tail_start, tail), :], w_tail, tail_sem)

    inputs = [pltpu.make_async_copy(src, dst, in_sem.at[i]) for i, (src, dst) in enumerate(
        ((h_hbm, h_ref), (draft_hbm, draft_ref), (temp_hbm, temp_ref), (gain_hbm, gain_ref)))]
    for copy in inputs:
        copy.start()
    for i in range(SLOTS):
        (own_tile if i < own else shared_tile)(i, i).start()

    barrier = pltpu.get_barrier_semaphore()
    peers = [{"dp": dp, "tp": lax.rem(me + k, tp)} for k in range(1, tp)]
    if pair:
        peers += [{"dp": mate, "tp": lax.rem(me + k, tp)} for k in range(tp)]
    for peer in peers:
        pl.semaphore_signal(barrier, inc=1, device_id=peer, device_id_type=MESH)

    for copy in inputs:
        copy.wait()
    norm_rows(h_ref, gain_ref, g_ref)

    lane = lax.broadcasted_iota(jnp.int32, (SUBS, LANES), 1)
    sub = lax.broadcasted_iota(jnp.int32, (SUBS, LANES), 0)
    drafts = draft_ref.shape[1]
    table_ref[...] = jnp.zeros((SUBS, LANES), jnp.float32)
    table_ref[0:batch, 0:drafts] = draft_ref[...].astype(jnp.float32)
    temps = jnp.ones((SUBS, LANES), jnp.float32)
    wants = jnp.full((SUBS, LANES), -1.0, jnp.float32)
    for b in range(batch):
        spread = jnp.broadcast_to(temp_ref[:, b:b + 1], (SUBS, LANES))
        ids = pltpu.roll(jnp.broadcast_to(table_ref[b:b + 1, :], (SUBS, LANES)), b * pos, 1)
        after = lane >= b * pos
        temps = jnp.where(after & (lane < b * pos + pos), spread, temps)
        wants = jnp.where(after & (lane < b * pos + drafts), ids, wants)
    table_ref[...] = jnp.where(sub == 0, temps, wants)
    pl.semaphore_wait(barrier, len(peers))

    trades, passes = [], []
    if pair:
        for j in range(batch // 2):
            b = 2 * j + core
            trades.append(pltpu.make_async_remote_copy(
                src_ref=g_ref.at[b], dst_ref=other_ref.at[b], send_sem=send_sem.at[j], recv_sem=recv_sem.at[j],
                device_id={"dp": mate, "tp": me}, device_id_type=MESH))
            passes.append(pltpu.make_async_remote_copy(
                src_ref=other_ref.at[b], dst_ref=other_ref.at[b], send_sem=pass_sem.at[j], recv_sem=got_sem.at[j],
                device_id={"dp": dp, "tp": twin}, device_id_type=MESH))
        trades.append(pltpu.make_async_remote_copy(
            src_ref=table_ref, dst_ref=other_table_ref, send_sem=send_sem.at[batch // 2],
            recv_sem=recv_sem.at[batch // 2], device_id={"dp": mate, "tp": me}, device_id_type=MESH))
        for copy in trades:
            copy.start()

    transpose_rows([g_ref], gt_ref)
    scale_ref[...] = 1.0 / temps
    want_ref[...] = wants.astype(jnp.int32)
    m_ref[...] = jnp.full((SUBS, LANES), LOW, jnp.float32)
    for ref in (s_ref, t_ref, p_ref):
        ref[...] = jnp.zeros((SUBS, LANES), jnp.float32)
    z_ref[...] = jnp.full(z_ref.shape, 2 * LOW, jnp.float32)

    def fold(width, first):
        fold_tile(z_ref, width, first, scale_ref[...], want_ref[...], m_ref, s_ref, t_ref, p_ref)

    def run_tiles(lo, hi, offset, before=None):
        first = me * rows + offset

        def step(i, _):
            slot = lax.rem(i, SLOTS)
            if before is not None:
                before(i)
            own_tile(0, slot).wait()
            fold(TILE, jnp.where(i > lo, first + (i - 1) * TILE, -(1 << 24)))
            z_ref[...] = jnp.dot(w_buf[slot], gt_ref[...], preferred_element_type=jnp.float32)

            @pl.when(i + SLOTS < own)
            def _():
                own_tile(i + SLOTS, slot).start()

            @pl.when((i + SLOTS >= own) & (i + SLOTS < n_full))
            def _():
                shared_tile(i + SLOTS, slot).start()

            @pl.when(i + SLOTS == n_full)
            def _():
                tail_copy.start()

            return 0

        lax.fori_loop(lo, hi, step, 0)
        fold(TILE, first + (hi - 1) * TILE)

    def pass_on(i):
        for j, at in enumerate(FORWARD_AT):
            @pl.when(i == at)
            def _(j=j):
                trades[j].wait_recv()
                passes[j].start()

    if pair:
        run_tiles(0, own, 0, pass_on)
        z_ref[...] = jnp.full(z_ref.shape, 2 * LOW, jnp.float32)
        mine = lane < used
        m_ref[...] = jnp.where(mine, m_ref[...], LOW)
        for ref in (s_ref, t_ref, p_ref):
            ref[...] = jnp.where(mine, ref[...], 0.0)
        trades[-1].wait_recv()
        both = jnp.where(mine, table_ref[...], pltpu.roll(other_table_ref[...], used, 1))
        temps = jnp.broadcast_to(both[0:1, :], (SUBS, LANES))
        wants = jnp.broadcast_to(both[1:2, :], (SUBS, LANES))
        scale_ref[...] = 1.0 / jnp.where(lane < 2 * used, temps, 1.0)
        want_ref[...] = jnp.where(lane < 2 * used, wants, -1.0).astype(jnp.int32)
        for copy in passes:
            copy.wait_recv()
        transpose_rows([g_ref, other_ref], gt_ref)
        run_tiles(own, n_full, skip)
    else:
        run_tiles(0, n_full, 0)

    tail_copy.wait()
    z_ref[0:tail, :] = jnp.dot(w_tail[...], gt_ref[...], preferred_element_type=jnp.float32)
    fold(tail, me * rows + tail_start)

    top = jnp.max(m_ref[...], axis=0, keepdims=True)
    weight = jnp.exp(m_ref[...] - top)
    total = jnp.sum(s_ref[...] * weight, axis=0, keepdims=True)
    weighted = jnp.sum(t_ref[...] * weight, axis=0, keepdims=True)
    picked = jnp.sum(p_ref[...], axis=0, keepdims=True)
    message = jnp.where(sub == 0, top, jnp.where(sub == 1, total, jnp.where(sub == 2, weighted, picked)))
    msg_ref[...] = message
    inbox_ref[me] = message
    sends = []
    for k, peer in enumerate(peers):
        slot = me if k < tp - 1 else me + tp
        sends.append(pltpu.make_async_remote_copy(
            src_ref=msg_ref, dst_ref=inbox_ref.at[slot], send_sem=out_sem.at[k], recv_sem=msg_sem.at[k],
            device_id=peer, device_id_type=MESH))
    for copy in sends:
        copy.start()
    for copy in trades + passes:
        copy.wait_send()
    for copy in sends:
        copy.wait()

    parts = [inbox_ref[k] for k in range(tp)]
    if pair:
        parts += [pltpu.roll(inbox_ref[tp + k], LANES - used, 1) for k in range(tp)]
    top = functools.reduce(jnp.maximum, [v[0:1, :] for v in parts])
    total = jnp.zeros((1, LANES), jnp.float32)
    weighted = total
    picked = total
    for v in parts:
        weight = jnp.exp(v[0:1, :] - top)
        total = total + v[1:2, :] * weight
        weighted = weighted + v[2:3, :] * weight
        picked = picked + v[3:4, :]
    log_norm = top + jnp.log(total)
    entropy = log_norm - weighted / total
    out = jnp.zeros((SUBS, LANES), jnp.float32)
    for n, row in enumerate((log_norm, entropy, picked - log_norm)):
        row = jnp.broadcast_to(row, (SUBS, LANES))
        for b in range(batch):
            here = (sub == b) & (lane >= n * pos) & (lane < (n + 1) * pos)
            out = jnp.where(here, pltpu.roll(row, (n * pos - b * pos) % LANES, 1), out)
    out_ref[...] = out


def solution(mesh):
    tp = mesh.shape["tp"]
    dp = mesh.shape["dp"]

    def local_step(hidden, draft_ids, temperature, norm_gain, head_shard):
        batch, pos, dim = hidden.shape
        rows = head_shard.shape[0]
        n_rows = batch * pos
        pair = PAIR and dp % 2 == 0 and batch % 2 == 0 and 2 * n_rows <= LANES
        own = OWN_TILES if pair else 0
        half = (rows - own * TILE) // (2 if pair else 1)
        sources = tp * (2 if pair else 1)
        row_block = pltpu.VMEM((batch, pos, dim), jnp.float32)
        stat = pltpu.VMEM((SUBS, LANES), jnp.float32)
        dma = pltpu.SemaphoreType.DMA
        hbm = pl.BlockSpec(memory_space=pltpu.HBM)
        small = [hidden.reshape(n_rows, dim), draft_ids, temperature.reshape(1, batch),
                 norm_gain.reshape(dim // LANES, LANES)]
        small = [pltpu.with_memory_space_constraint(x, pltpu.HBM) for x in small]
        out = pl.pallas_call(
            functools.partial(kernel, tp, pair, batch, pos, own, half),
            out_shape=jax.ShapeDtypeStruct((SUBS, LANES), jnp.float32),
            in_specs=[hbm] * 5,
            out_specs=pl.BlockSpec(memory_space=pltpu.VMEM),
            scratch_shapes=[
                pltpu.VMEM((n_rows, dim), jnp.bfloat16),
                pltpu.VMEM(draft_ids.shape, jnp.int32),
                pltpu.VMEM((1, batch), jnp.float32),
                pltpu.VMEM((dim // LANES, LANES), jnp.bfloat16),
                stat,
                stat,
                row_block,
                row_block,
                pltpu.VMEM((dim, LANES), jnp.bfloat16),
                pltpu.VMEM((SLOTS, TILE, dim), jnp.bfloat16),
                pltpu.VMEM((half % TILE, dim), jnp.bfloat16),
                pltpu.VMEM((TILE, LANES), jnp.float32),
                stat,
                pltpu.VMEM((SUBS, LANES), jnp.int32),
                stat, stat, stat, stat,
                stat,
                pltpu.VMEM((sources, SUBS, LANES), jnp.float32),
                dma((4,)),
                dma((SLOTS,)),
                dma,
                dma((batch // 2 + 1,)),
                dma((batch // 2 + 1,)),
                dma((batch // 2,)),
                dma((batch // 2,)),
                dma((sources - 1,)),
                dma((sources - 1,)),
            ],
            compiler_params=pltpu.CompilerParams(
                collective_id=0, has_side_effects=True, vmem_limit_bytes=50 * 1024 * 1024),
        )(*small, head_shard)
        return out[:batch, 2 * pos:3 * pos - 1], out[:batch, :pos], out[:batch, pos:2 * pos]

    return jax.shard_map(
        local_step,
        mesh=mesh,
        in_specs=(P("dp", None, None), P("dp", None), P("dp"), P(None), P("tp", None)),
        out_specs=(P("dp", None), P("dp", None), P("dp", None)),
        check_vma=False,
    )
```

time: 2920 us -> 49.9 us (0.02)
  waiting for transfers between devices: 2220 us -> 0 us
  other arithmetic: 335 us -> 0 us
  local copies, waits for them, and re-layouts: 291 us -> 1.33 us
  matrix products: 48.6 us -> 0 us
  Pallas kernels: 0 us -> 47.8 us
    all_gather x1 -> x0, waiting for transfers between devices: 2220 us -> none  [local_step(): logits = lax.all_gather(shard_logits, 'tp', axis=2, tiled=True)]
    unnamed x13 -> x0, local copies, waits for them, and re-layouts: 258 us -> none
    reduce_sum x2 -> x0, other arithmetic: 177 us -> none  [the longest x1 175 us: local_step(): weighted = jnp.sum(shifted * logits, axis=-1)]
    reduce_max x1 -> x0, other arithmetic: 157 us -> none  [local_step(): row_max = jnp.max(logits, axis=-1, keepdims=True)]
    dot_general x1 -> x0, matrix products: 48.6 us -> none  [local_step(): jnp.einsum('bpd,vd->bpv', normed, head_shard, preferred_element_type=jnp....]
    pallas_call x0 -> x1, Pallas kernels: none -> 47.8 us  [local_step(): pl.pallas_call(functools.partial(kernel, tp, pair, batch, pos, own, half)...]
    div x1 -> x0, local copies, waits for them, and re-layouts: 29.7 us -> none  [local_step(): shard_logits = shard_logits / value_a11[:, None, None]]
  transfers between devices with their start and end apart: 1 -> 0, of which waited for: 1 -> 0; matrix products, arithmetic and copies ran while one was open for 0% -> 0% of each run, Pallas kernels for 0% -> 0%
where the time goes in v2:
time: 49.9 us; the launch traced here: 49.8 us
  Pallas kernels  47.8 us (96%)
  local copies, waits for them, and re-layouts  1.33 us (3%)
  between operations  0.64 us (1%)
    pallas_call x1, Pallas kernels, local_step(): pl.pallas_call(functools.partial(kernel, tp, pair, batch, pos, own, half)...  47.8 us

profile of v2, /device:TPU:81, one launch (start us, length us, event | category | flops | bytes accessed | tf_op | source)
XLA Modules:
  0.0 49.8 jit_solution(1008273269346336602)
XLA Ops:
  0.6 47.8 %shard_map.76 = f32[8,128]{1,0:T(8,128)S(1)} custom-call(bf16[48,4096]{1,0:T(8,128)(2,1)} %bitcast.3, s32[6,7]{1,0:T(8,128)} %draft_hbm.1, f32[1,6]{1,0:T(1,128)} %bitcast.5, bf16[32,128]{1,0:T(8,128)(2,1)} %bitcast.4, bf16[16032,4096]{1,0:T(8,128)(2,1)} %w_ref.1), custom_call_target="tpu_custom_call" | custom-call | tf_op jit(solution)/shard_map/pallas_call | solution.py:284
  48.5 0.7 %fusion = (f32[6,8]{1,0:T(8,128)}, f32[6,8]{1,0:T(8,128)}) fusion(f32[8,128]{1,0:T(8,128)S(1)} %shard_map.76), kind=kLoop, calls=%fused_computation | loop fusion | bytes 768 | tf_op jit(solution)/shard_map/slice | solution.py:320
  49.1 0.7 %slice.9 = f32[6,7]{1,0:T(8,128)} slice(f32[8,128]{1,0:T(8,128)S(1)} %shard_map.76), slice={[0:6], [16:23]} | slice | bytes 336 | tf_op jit(solution)/shard_map/slice | solution.py:320

commit v3 on v2

--- a/solution.py
+++ b/solution.py
@@ -10,7 +10,8 @@
 NORM_EPS = 1e-5
 PAIR = True
 TILE = 512
-SLOTS = 10
+SLOTS = 4
+EARLY = 2
 OWN_TILES = 9
 FORWARD_AT = (4, 6, 8)
 LANES = 128
@@ -102,7 +103,7 @@
         ((h_hbm, h_ref), (draft_hbm, draft_ref), (temp_hbm, temp_ref), (gain_hbm, gain_ref)))]
     for copy in inputs:
         copy.start()
-    for i in range(SLOTS):
+    for i in range(EARLY):
         (own_tile if i < own else shared_tile)(i, i).start()
 
     barrier = pltpu.get_barrier_semaphore()
@@ -148,6 +149,8 @@
         for copy in trades:
             copy.start()
 
+    for i in range(EARLY, SLOTS):
+        (own_tile if i < own else shared_tile)(i, i).start()
     transpose_rows([g_ref], gt_ref)
     scale_ref[...] = 1.0 / temps
     want_ref[...] = wants.astype(jnp.int32)

time: 49.9 us -> 40.2 us (0.81)
  Pallas kernels: 47.8 us -> 38.2 us
    pallas_call x1, Pallas kernels: 47.8 us -> 38.2 us  [local_step(): pl.pallas_call(functools.partial(kernel, tp, pair, batch, pos, own, half)...]
where the time goes in v3:
time: 40.2 us
  Pallas kernels  38.2 us (95%)
  local copies, waits for them, and re-layouts  1.33 us (3%)
  between operations  0.64 us (2%)
    pallas_call x1, Pallas kernels, local_step(): pl.pallas_call(functools.partial(kernel, tp, pair, batch, pos, own, half)...  38.2 us

profile of v3, /device:TPU:81, one launch (start us, length us, event | category | flops | bytes accessed | tf_op | source)
XLA Modules:
  0.0 40.2 jit_solution(16684314142630294264)
XLA Ops:
  0.6 38.2 %shard_map.76 = f32[8,128]{1,0:T(8,128)S(1)} custom-call(bf16[48,4096]{1,0:T(8,128)(2,1)} %bitcast.3, s32[6,7]{1,0:T(8,128)} %draft_hbm.1, f32[1,6]{1,0:T(1,128)} %bitcast.5, bf16[32,128]{1,0:T(8,128)(2,1)} %bitcast.4, bf16[16032,4096]{1,0:T(8,128)(2,1)} %w_ref.1), custom_call_target="tpu_custom_call" | custom-call | tf_op jit(solution)/shard_map/pallas_call | solution.py:287
  38.8 0.7 %fusion = (f32[6,8]{1,0:T(8,128)}, f32[6,8]{1,0:T(8,128)}) fusion(f32[8,128]{1,0:T(8,128)S(1)} %shard_map.76), kind=kLoop, calls=%fused_computation | loop fusion | bytes 768 | tf_op jit(solution)/shard_map/slice | solution.py:323
  39.5 0.7 %slice.9 = f32[6,7]{1,0:T(8,128)} slice(f32[8,128]{1,0:T(8,128)S(1)} %shard_map.76), slice={[0:6], [16:23]} | slice | bytes 336 | tf_op jit(solution)/shard_map/slice | solution.py:323

commit v4 on v3

--- a/solution.py
+++ b/solution.py
@@ -10,9 +10,9 @@
 NORM_EPS = 1e-5
 PAIR = True
 TILE = 512
-SLOTS = 4
-EARLY = 2
-OWN_TILES = 9
+SLOTS = 3
+EARLY = 1
+OWN_TILES = 11
 FORWARD_AT = (4, 6, 8)
 LANES = 128
 SUBS = 8
@@ -263,6 +263,14 @@
             here = (sub == b) & (lane >= n * pos) & (lane < (n + 1) * pos)
             out = jnp.where(here, pltpu.roll(row, (n * pos - b * pos) % LANES, 1), out)
     out_ref[...] = out
+
+
+def spread(packed_ref, lp_ref, lse_ref, ent_ref):
+    batch, pos = lse_ref.shape
+    packed = packed_ref[...]
+    lse_ref[...] = packed[:batch, :pos]
+    ent_ref[...] = packed[:batch, pos:2 * pos]
+    lp_ref[...] = packed[:batch, 2 * pos:3 * pos - 1]
 
 
 def solution(mesh):
@@ -320,7 +328,15 @@
             compiler_params=pltpu.CompilerParams(
                 collective_id=0, has_side_effects=True, vmem_limit_bytes=50 * 1024 * 1024),
         )(*small, head_shard)
-        return out[:batch, 2 * pos:3 * pos - 1], out[:batch, :pos], out[:batch, pos:2 * pos]
+        vmem = pl.BlockSpec(memory_space=pltpu.VMEM)
+        shapes = ((batch, pos - 1), (batch, pos), (batch, pos))
+        return pl.pallas_call(
+            spread,
+            out_shape=tuple(jax.ShapeDtypeStruct(shape, jnp.float32) for shape in shapes),
+            in_specs=[vmem],
+            out_specs=(vmem, vmem, vmem),
+            compiler_params=pltpu.CompilerParams(vmem_limit_bytes=1 << 20),
+        )(out)
 
     return jax.shard_map(
         local_step,

time: 40.2 us -> 40.8 us (1.015)
  Pallas kernels: 38.2 us -> 40.1 us
  local copies, waits for them, and re-layouts: 1.33 us -> 0 us
    slice x2 -> x0, local copies, waits for them, and re-layouts: 1.33 us -> none  [the longest x1 0.67 us: local_step(): out[:batch, pos:2 * pos]]
    pallas_call x1, Pallas kernels: 38.2 us -> 39.4 us  [local_step(): pl.pallas_call(functools.partial(kernel, tp, pair, batch, pos, own, half)...]
    pallas_call x0 -> x1, Pallas kernels: none -> 0.67 us  [local_step(): pl.pallas_call(spread, out_shape=tuple((jax.ShapeDtypeStruct(shape, jnp.f...]
where the time goes in v4:
time: 40.8 us; the launch traced here: 40.7 us
  Pallas kernels  40.1 us (98%)
  between operations  0.64 us (2%)
    pallas_call x1, Pallas kernels, local_step(): pl.pallas_call(functools.partial(kernel, tp, pair, batch, pos, own, half)...  39.4 us

profile of v4, /device:TPU:81, one launch (start us, length us, event | category | flops | bytes accessed | tf_op | source)
XLA Modules:
  0.0 40.7 jit_solution(7993398051502215542)
XLA Ops:
  0.6 39.4 %shard_map.76.packed_ref = f32[8,128]{1,0:T(8,128)S(1)} custom-call(bf16[48,4096]{1,0:T(8,128)(2,1)} %bitcast.3, s32[6,7]{1,0:T(8,128)} %draft_hbm.1, f32[1,6]{1,0:T(1,128)} %bitcast.5, bf16[32,128]{1,0:T(8,128)(2,1)} %bitcast.4, bf16[16032,4096]{1,0:T(8,128)(2,1)} %w_ref.1), custom_call_target="tpu_custom_call" | custom-call | tf_op jit(solution)/shard_map/pallas_call | solution.py:295
  40.0 0.7 %shard_map.77 = (f32[6,7]{1,0:T(8,128)}, f32[6,8]{1,0:T(8,128)}, f32[6,8]{1,0:T(8,128)}) custom-call(f32[8,128]{1,0:T(8,128)S(1)} %shard_map.76.packed_ref), custom_call_target="tpu_custom_call" | custom-call | tf_op jit(solution)/shard_map/pallas_call | solution.py:333

commit v5 on v4

--- a/solution.py
+++ b/solution.py
@@ -10,9 +10,11 @@
 NORM_EPS = 1e-5
 PAIR = True
 TILE = 512
-SLOTS = 3
-EARLY = 1
-OWN_TILES = 11
+SLOTS = 4
+EARLY = 2
+OWN_TILES = 9
+BIG = 2 * TILE
+BIG_SLOTS = 3
 FORWARD_AT = (4, 6, 8)
 LANES = 128
 SUBS = 8
@@ -74,9 +76,9 @@
 
 
 def kernel(tp, pair, batch, pos, own, half, h_hbm, draft_hbm, temp_hbm, gain_hbm, w_ref, out_ref,
-           h_ref, draft_ref, temp_ref, gain_ref, table_ref, other_table_ref, g_ref, other_ref, gt_ref, w_buf, w_tail, z_ref,
+           h_ref, draft_ref, temp_ref, gain_ref, table_ref, other_table_ref, g_ref, other_ref, gt_ref, w_buf, big_buf, w_tail, z_ref,
            scale_ref, want_ref, m_ref, s_ref, t_ref, p_ref, msg_ref, inbox_ref,
-           in_sem, w_sem, tail_sem, send_sem, recv_sem, pass_sem, got_sem, out_sem, msg_sem):
+           in_sem, w_sem, big_sem, tail_sem, send_sem, recv_sem, pass_sem, got_sem, out_sem, msg_sem):
     rows = w_ref.shape[0]
     used = batch * pos
     me = lax.axis_index("tp")
@@ -84,27 +86,29 @@
     mate = dp + 1 - 2 * lax.rem(dp, 2)
     core = lax.rem(me, 2)
     twin = me + 1 - 2 * core
-    n_full = own + half // TILE
-    tail = half % TILE
-    skip = lax.rem(dp, 2) * half if pair else 0
+    n_big = half // BIG
+    tail = half % BIG
+    shared = own * TILE + (lax.rem(dp, 2) * half if pair else 0)
 
     def own_tile(i, slot):
         start = pl.multiple_of(i * TILE, TILE)
         return pltpu.make_async_copy(w_ref.at[pl.ds(start, TILE), :], w_buf.at[slot], w_sem.at[slot])
 
-    def shared_tile(i, slot):
-        start = pl.multiple_of(i * TILE + skip, 16)
-        return pltpu.make_async_copy(w_ref.at[pl.ds(start, TILE), :], w_buf.at[slot], w_sem.at[slot])
-
-    tail_start = pl.multiple_of(n_full * TILE + skip, 16)
+    def big_piece(i, slot, k):
+        start = pl.multiple_of(shared + i * BIG + k * TILE, 16)
+        return pltpu.make_async_copy(
+            w_ref.at[pl.ds(start, TILE), :], big_buf.at[slot, pl.ds(k * TILE, TILE), :], big_sem.at[slot, k])
+
+    tail_start = pl.multiple_of(shared + n_big * BIG, 16)
     tail_copy = pltpu.make_async_copy(w_ref.at[pl.ds(tail_start, tail), :], w_tail, tail_sem)
 
     inputs = [pltpu.make_async_copy(src, dst, in_sem.at[i]) for i, (src, dst) in enumerate(
         ((h_hbm, h_ref), (draft_hbm, draft_ref), (temp_hbm, temp_ref), (gain_hbm, gain_ref)))]
     for copy in inputs:
         copy.start()
-    for i in range(EARLY):
-        (own_tile if i < own else shared_tile)(i, i).start()
+    if pair:
+        for i in range(EARLY):
+            own_tile(i, i).start()
 
     barrier = pltpu.get_barrier_semaphore()
     peers = [{"dp": dp, "tp": lax.rem(me + k, tp)} for k in range(1, tp)]
@@ -149,8 +153,11 @@
         for copy in trades:
             copy.start()
 
-    for i in range(EARLY, SLOTS):
-        (own_tile if i < own else shared_tile)(i, i).start()
+        for i in range(EARLY, SLOTS):
+            own_tile(i, i).start()
+    else:
+        for q in range(SLOTS):
+            big_piece(q // 2, q // 2, q % 2).start()
     transpose_rows([g_ref], gt_ref)
     scale_ref[...] = 1.0 / temps
     want_ref[...] = wants.astype(jnp.int32)
@@ -162,33 +169,48 @@
     def fold(width, first):
         fold_tile(z_ref, width, first, scale_ref[...], want_ref[...], m_ref, s_ref, t_ref, p_ref)
 
-    def run_tiles(lo, hi, offset, before=None):
-        first = me * rows + offset
-
-        def step(i, _):
-            slot = lax.rem(i, SLOTS)
-            if before is not None:
-                before(i)
-            own_tile(0, slot).wait()
-            fold(TILE, jnp.where(i > lo, first + (i - 1) * TILE, -(1 << 24)))
-            z_ref[...] = jnp.dot(w_buf[slot], gt_ref[...], preferred_element_type=jnp.float32)
-
-            @pl.when(i + SLOTS < own)
-            def _():
-                own_tile(i + SLOTS, slot).start()
-
-            @pl.when((i + SLOTS >= own) & (i + SLOTS < n_full))
-            def _():
-                shared_tile(i + SLOTS, slot).start()
-
-            @pl.when(i + SLOTS == n_full)
-            def _():
-                tail_copy.start()
-
-            return 0
-
-        lax.fori_loop(lo, hi, step, 0)
-        fold(TILE, first + (hi - 1) * TILE)
+    none = -(1 << 24)
+
+    def third_tile():
+        for i in range(SLOTS // 2, BIG_SLOTS):
+            for k in range(2):
+                big_piece(i, i, k).start()
+
+    def own_step(i, _):
+        slot = lax.rem(i, SLOTS)
+        pass_on(i)
+        own_tile(0, slot).wait()
+        fold(TILE, jnp.where(i > 0, me * rows + (i - 1) * TILE, none))
+        z_ref[0:TILE, :] = jnp.dot(w_buf[slot], gt_ref[...], preferred_element_type=jnp.float32)
+
+        @pl.when(i + SLOTS < own)
+        def _():
+            own_tile(i + SLOTS, slot).start()
+
+        for q in range(SLOTS):
+            @pl.when(i == own - SLOTS + q)
+            def _(q=q):
+                big_piece(q // 2, q // 2, q % 2).start()
+
+        return 0
+
+    def big_step(i, _):
+        slot = lax.rem(i, BIG_SLOTS)
+        for k in range(2):
+            big_piece(0, slot, k).wait()
+        fold(BIG, jnp.where(i > 0, me * rows + shared + (i - 1) * BIG, none))
+        z_ref[...] = jnp.dot(big_buf[slot], gt_ref[...], preferred_element_type=jnp.float32)
+
+        @pl.when(i + BIG_SLOTS < n_big)
+        def _():
+            for k in range(2):
+                big_piece(i + BIG_SLOTS, slot, k).start()
+
+        @pl.when(i + BIG_SLOTS == n_big)
+        def _():
+            tail_copy.start()
+
+        return 0
 
     def pass_on(i):
         for j, at in enumerate(FORWARD_AT):
@@ -198,7 +220,8 @@
                 passes[j].start()
 
     if pair:
-        run_tiles(0, own, 0, pass_on)
+        lax.fori_loop(0, own, own_step, 0)
+        fold(TILE, me * rows + (own - 1) * TILE)
         z_ref[...] = jnp.full(z_ref.shape, 2 * LOW, jnp.float32)
         mine = lane < used
         m_ref[...] = jnp.where(mine, m_ref[...], LOW)
@@ -212,11 +235,14 @@
         want_ref[...] = jnp.where(lane < 2 * used, wants, -1.0).astype(jnp.int32)
         for copy in passes:
             copy.wait_recv()
+        third_tile()
         transpose_rows([g_ref, other_ref], gt_ref)
-        run_tiles(own, n_full, skip)
+
     else:
-        run_tiles(0, n_full, 0)
-
+        third_tile()
+
+    lax.fori_loop(0, n_big, big_step, 0)
+    fold(BIG, me * rows + shared + (n_big - 1) * BIG)
     tail_copy.wait()
     z_ref[0:tail, :] = jnp.dot(w_tail[...], gt_ref[...], preferred_element_type=jnp.float32)
     fold(tail, me * rows + tail_start)
@@ -308,8 +334,9 @@
                 row_block,
                 pltpu.VMEM((dim, LANES), jnp.bfloat16),
                 pltpu.VMEM((SLOTS, TILE, dim), jnp.bfloat16),
-                pltpu.VMEM((half % TILE, dim), jnp.bfloat16),
-                pltpu.VMEM((TILE, LANES), jnp.float32),
+                pltpu.VMEM((BIG_SLOTS, BIG, dim), jnp.bfloat16),
+                pltpu.VMEM((half % BIG, dim), jnp.bfloat16),
+                pltpu.VMEM((BIG, LANES), jnp.float32),
                 stat,
                 pltpu.VMEM((SUBS, LANES), jnp.int32),
                 stat, stat, stat, stat,
@@ -317,6 +344,7 @@
                 pltpu.VMEM((sources, SUBS, LANES), jnp.float32),
                 dma((4,)),
                 dma((SLOTS,)),
+                dma((BIG_SLOTS, 2)),
                 dma,
                 dma((batch // 2 + 1,)),
                 dma((batch // 2 + 1,)),

time: 40.8 us -> 38.8 us (0.951)
  Pallas kernels: 40.1 us -> 38.1 us
    pallas_call x1, Pallas kernels: 39.4 us -> 37.4 us  [local_step(): pl.pallas_call(functools.partial(kernel, tp, pair, batch, pos, own, half)...]
where the time goes in v5:
time: 38.8 us; the launch traced here: 38.7 us
  Pallas kernels  38.1 us (98%)
  between operations  0.64 us (2%)
    pallas_call x1, Pallas kernels, local_step(): pl.pallas_call(functools.partial(kernel, tp, pair, batch, pos, own, half)...  37.4 us

profile of v5, /device:TPU:81, one launch (start us, length us, event | category | flops | bytes accessed | tf_op | source)
XLA Modules:
  0.0 38.7 jit_solution(10841240736224300394)
XLA Ops:
  0.6 37.4 %shard_map.76.packed_ref = f32[8,128]{1,0:T(8,128)S(1)} custom-call(bf16[48,4096]{1,0:T(8,128)(2,1)} %bitcast.3, s32[6,7]{1,0:T(8,128)} %draft_hbm.1, f32[1,6]{1,0:T(1,128)} %bitcast.5, bf16[32,128]{1,0:T(8,128)(2,1)} %bitcast.4, bf16[16032,4096]{1,0:T(8,128)(2,1)} %w_ref.1), custom_call_target="tpu_custom_call" | custom-call | tf_op jit(solution)/shard_map/pallas_call | solution.py:321
  38.1 0.7 %shard_map.77 = (f32[6,7]{1,0:T(8,128)}, f32[6,8]{1,0:T(8,128)}, f32[6,8]{1,0:T(8,128)}) custom-call(f32[8,128]{1,0:T(8,128)S(1)} %shard_map.76.packed_ref), custom_call_target="tpu_custom_call" | custom-call | tf_op jit(solution)/shard_map/pallas_call | solution.py:361

commit v6 on v5

--- a/solution.py
+++ b/solution.py
@@ -11,11 +11,11 @@
 PAIR = True
 TILE = 512
 SLOTS = 4
-EARLY = 2
-OWN_TILES = 9
+EARLY = 1
+OWN_TILES = 7
 BIG = 2 * TILE
 BIG_SLOTS = 3
-FORWARD_AT = (4, 6, 8)
+FORWARD_AT = (3, 5, 6)
 LANES = 128
 SUBS = 8
 LOW = -1e30
@@ -171,7 +171,7 @@
 
     none = -(1 << 24)
 
-    def third_tile():
+    def run_ahead():
         for i in range(SLOTS // 2, BIG_SLOTS):
             for k in range(2):
                 big_piece(i, i, k).start()
@@ -191,6 +191,10 @@
             @pl.when(i == own - SLOTS + q)
             def _(q=q):
                 big_piece(q // 2, q // 2, q % 2).start()
+
+        @pl.when(i == own - 1)
+        def _():
+            run_ahead()
 
         return 0
 
@@ -235,11 +239,10 @@
         want_ref[...] = jnp.where(lane < 2 * used, wants, -1.0).astype(jnp.int32)
         for copy in passes:
             copy.wait_recv()
-        third_tile()
         transpose_rows([g_ref, other_ref], gt_ref)
 
     else:
-        third_tile()
+        run_ahead()
 
     lax.fori_loop(0, n_big, big_step, 0)
     fold(BIG, me * rows + shared + (n_big - 1) * BIG)

time: 38.8 us -> 39.6 us (1.021)
  Pallas kernels: 38.1 us -> 38.9 us
    pallas_call x1, Pallas kernels: 37.4 us -> 38.2 us  [local_step(): pl.pallas_call(functools.partial(kernel, tp, pair, batch, pos, own, half)...]
where the time goes in v6:
time: 39.6 us; the launch traced here: 39.5 us
  Pallas kernels  38.9 us (98%)
  between operations  0.64 us (2%)
    pallas_call x1, Pallas kernels, local_step(): pl.pallas_call(functools.partial(kernel, tp, pair, batch, pos, own, half)...  38.2 us

profile of v6, /device:TPU:81, one launch (start us, length us, event | category | flops | bytes accessed | tf_op | source)
XLA Modules:
  0.0 39.5 jit_solution(2422003418215639888)
XLA Ops:
  0.6 38.2 %shard_map.76.packed_ref = f32[8,128]{1,0:T(8,128)S(1)} custom-call(bf16[48,4096]{1,0:T(8,128)(2,1)} %bitcast.3, s32[6,7]{1,0:T(8,128)} %draft_hbm.1, f32[1,6]{1,0:T(1,128)} %bitcast.5, bf16[32,128]{1,0:T(8,128)(2,1)} %bitcast.4, bf16[16032,4096]{1,0:T(8,128)(2,1)} %w_ref.1), custom_call_target="tpu_custom_call" | custom-call | tf_op jit(solution)/shard_map/pallas_call | solution.py:324
  38.9 0.7 %shard_map.77 = (f32[6,7]{1,0:T(8,128)}, f32[6,8]{1,0:T(8,128)}, f32[6,8]{1,0:T(8,128)}) custom-call(f32[8,128]{1,0:T(8,128)S(1)} %shard_map.76.packed_ref), custom_call_target="tpu_custom_call" | custom-call | tf_op jit(solution)/shard_map/pallas_call | solution.py:364
